TPU v7x, 256 devices: a whole 4x4x8 slice. The times are simulated.
256 devices in a mesh: layer: 4 (over z_lo, core), feat: 64 (over y, z_hi, x).
Axes of the slice: x: 4, y: 4, z: 8 (z_hi: 4, z_lo: 2; z = z_hi * 2 + z_lo), core: 2. Of those that a mesh axis runs over, the one named last changes fastest.
Arguments:
- activations: bfloat16 [512, 4, 2304], P('feat', 'layer'), may hold values from -6 to 6
- enc_weight: bfloat16 [4, 2304, 65536], P('layer', None, 'feat'), may hold values from -0.0625 to 0.0625
- dec_weight: bfloat16 [4, 65536, 2304], P('layer', 'feat'), may hold values from -0.03125 to 0.03125
- enc_bias: float32 [65536], P('feat'), may hold values from -3 to 3
- threshold: float32 [65536], P('feat'), may hold values from 0.1 to 1
- dec_bias: float32 [4, 2304], P('layer'), may hold values from -3 to 3
- token_mask: int32 [512], replicated, may hold values 0 or 1
Outputs:
- squared_error: float32 [512, 4], P('feat', 'layer')
- latent_grad: float32 [512, 65536], P(None, 'feat')
- input_grad: bfloat16 [512, 4, 2304], P('feat', 'layer')
All inputs are finite; a program needn't handle non-finite values.
Results may differ from a plain program's by a relative error of at most 0.015.
Values may be sent and summed in bfloat16 or wider, within the bound.
A program may use at most 64 MiB of HBM per device.

v0:
```python
import jax
import jax.numpy as jnp
from jax import lax
from jax.sharding import Mesh
from jax.sharding import PartitionSpec as P

FEAT = ("feat_0", "feat_1", "feat_2")
jump_scale = 0.25


def split_up(array, dim, length):
    before, after = (array.shape[:dim], array.shape[dim + 1 :])
    return jnp.moveaxis(array.reshape(*before, length, -1, *after), dim, 0)


def sent_and_summed(array, axis, dim):
    length = lax.axis_size(axis)
    parts = lax.all_to_all(split_up(array, dim, length), axis, 0, 0, tiled=True)
    return jnp.sum(parts, axis=0)


def sum_by_axis(array, axes, dim):
    far, near = axes
    parts = split_up(array, dim, lax.axis_size(far))
    nearer = sent_and_summed(parts, near, dim + 1)
    arrived = lax.all_to_all(nearer, far, split_axis=0, concat_axis=0, tiled=True)
    return arrived.sum(axis=0)


def shards(activations, enc_weight, dec_weight, enc_bias, threshold, dec_bias, token_mask):
    tok_dev = activations.shape[0]
    partial_value = jnp.einsum(
        "tld,ldf->tf",
        lax.all_gather(activations, FEAT, axis=0, tiled=True),
        enc_weight,
        preferred_element_type=jnp.float32,
    )
    preact = lax.psum(partial_value.astype(jnp.bfloat16), "layer").astype(jnp.float32) + enc_bias
    gating = jax.nn.sigmoid((preact - threshold) / jump_scale)
    latent = (preact * gating).astype(jnp.bfloat16)
    gate_slope = gating + preact * gating * (1.0 - gating) / jump_scale
    first_row = lax.axis_index(FEAT) * tok_dev
    rows = latent
    rebuilt = sum_by_axis(
        jnp.einsum("tf,lfd->tld", rows, dec_weight, preferred_element_type=jnp.float32),
        (("feat_0", "feat_1"), "feat_2"),
        0,
    )
    own_mask = lax.dynamic_slice_in_dim(token_mask, first_row, tok_dev, 0).astype(jnp.float32)[
        :, None, None
    ]
    error = own_mask * (rebuilt + dec_bias[None, :, :] - activations.astype(jnp.float32))
    grad_part = jnp.einsum(
        "tld,lfd->tf",
        lax.all_gather(error.astype(jnp.bfloat16), FEAT, axis=0, tiled=True),
        dec_weight,
        preferred_element_type=jnp.float32,
    )
    squared_error = jnp.mean(error * error, axis=-1)
    latent_grad = lax.psum(grad_part.astype(jnp.bfloat16), "layer").astype(jnp.float32)
    preact_grad = (latent_grad * gate_slope).astype(jnp.bfloat16)
    rows = preact_grad
    grad_terms = sum_by_axis(
        jnp.einsum("tf,ldf->tld", rows, enc_weight, preferred_element_type=jnp.float32),
        (("feat_0", "feat_1"), "feat_2"),
        0,
    )
    input_grad = (grad_terms - error).astype(jnp.bfloat16)
    return (squared_error, latent_grad, input_grad)


def solution(mesh):
    finer = Mesh(
        mesh.devices.reshape(mesh.shape["layer"], 4, 4, 4), ("layer", "feat_0", "feat_1", "feat_2")
    )
    return jax.shard_map(
        shards,
        mesh=finer,
        in_specs=(
            P(FEAT, "layer", None),
            P("layer", None, FEAT),
            P("layer", FEAT, None),
            P(FEAT),
            P(FEAT),
            P("layer", None),
            P(),
        ),
        out_specs=(P(FEAT, "layer"), P(None, FEAT), P(FEAT, "layer", None)),
        check_vma=False,
    )
```

profile of v0, /device:TPU:32, one launch (start us, length us, event | category | flops | bytes accessed | tf_op | source)
XLA Modules:
  0.0 498.0 jit_solution(7002110068138016690)
XLA Ops:
  7.2 0.7 all-gather.3.cloned.1.call-update
  8.0 84.0 %all-gather.3.cloned.1.call-done = bf16[512,1,2304]{2,0,1:T(8,128)(2,1)} async-done(((bf16[8,1,2304]{2,0,1:T(8,128)(2,1)}), bf16[512,1,2304]{2,0,1:T(8,128)(2,1)}) %all-gather.3.cloned.1.call-update) | async-done | bytes 2359312 | tf_op jit(solution)/shard_map/all_gather | solution.py:34
  91.9 6.6 %fusion.10 = bf16[512,1024]{1,0:T(8,128)(2,1)} fusion(bf16[1,2304,1024]{2,1,0:T(8,128)(2,1)} %param.8, bf16[512,1,2304]{2,0,1:T(8,128)(2,1)} %all-gather.3.cloned.1.call-done), kind=kOutput, calls=%fused_computation.15 | convolution fusion | flops 2416443392 | bytes 8126464 | tf_op jit(solution)/shard_map/tld,ldf->tf/dot_general | solution.py:32
  98.6 44.8 %all-reduce.3.cloned.1.call-done = bf16[512,1024]{1,0:T(8,128)(2,1)} async-done(((bf16[512,1024]{1,0:T(8,128)(2,1)}), bf16[512,1024]{1,0:T(8,128)(2,1)}) %all-reduce.3.cloned.1.call-update) | async-done | bytes 1048592 | tf_op jit(solution)/shard_map/psum | solution.py:38
  143.4 1.9 fusion.9
  145.3 4.9 convolution_bitcast_fusion.1
  150.2 0.4 copy.10
  150.6 58.9 %all_to_all.20 = f32[4,16,8,1,2304]{4,2,1,3,0:T(8,128)} all-to-all(f32[4,16,8,1,2304]{4,2,1,3,0:T(8,128)S(1)} %copy.10), channel_id=1, replica_groups=mesh['layer'=4,'feat_0'=4,'feat_1'=4,'feat_2'=4] {'feat_2'}, dimensions={0} | all-to-all | bytes 9437184 | tf_op jit(solution)/shard_map/all_to_all | solution.py:18
  209.6 3.7 reduce_sum.53
  213.3 9.2 %all-to-all-start.1 = ((f32[16,8,1,2304]{3,1,2,0:T(8,128)}), f32[16,8,1,2304]{3,1,2,0:T(8,128)S(1)}, u32[]{:S(2)}, u32[]{:S(2)}) async-start(f32[16,8,1,2304]{3,1,2,0:T(8,128)} %bitcast.8), calls=%async_computation.1 | async-start | bytes 2359296 | tf_op jit(solution)/shard_map/all_to_all | solution.py:26
  222.6 0.8 dynamic-slice_convert_fusion
  223.4 31.0 %all-to-all-done.1 = f32[16,8,1,2304]{3,1,2,0:T(8,128)S(1)} async-done(((f32[16,8,1,2304]{3,1,2,0:T(8,128)}), f32[16,8,1,2304]{3,1,2,0:T(8,128)S(1)}, u32[]{:S(2)}, u32[]{:S(2)}) %all-to-all-start.1) | async-done | bytes 1179680 | tf_op jit(solution)/shard_map/all_to_all | solution.py:26
  254.5 0.7 fusion.23
  255.5 71.8 %all-gather.5.cloned.1.call-done = bf16[512,1,2304]{2,0,1:T(8,128)(2,1)} async-done(((bf16[8,1,2304]{2,0,1:T(8,128)(2,1)}), bf16[512,1,2304]{2,0,1:T(8,128)(2,1)}) %all-gather.5.cloned.1.call-update) | async-done | bytes 2359312 | tf_op jit(solution)/shard_map/all_gather | solution.py:55
  327.3 6.7 %fusion.15 = bf16[512,1024]{1,0:T(8,128)(2,1)} fusion(bf16[1,1024,2304]{2,1,0:T(8,128)(2,1)} %param.9, bf16[512,1,2304]{2,0,1:T(8,128)(2,1)} %all-gather.5.cloned.1.call-done), kind=kOutput, calls=%fused_computation.16 | convolution fusion | flops 2416443392 | bytes 8126464 | tf_op jit(solution)/shard_map/tld,lfd->tf/dot_general | solution.py:53
  333.9 44.7 %all-reduce.5.cloned.1.call-done = bf16[512,1024]{1,0:T(8,128)(2,1)} async-done(((bf16[512,1024]{1,0:T(8,128)(2,1)}), bf16[512,1024]{1,0:T(8,128)(2,1)}) %all-reduce.5.cloned.1.call-update) | async-done | bytes 1048592 | tf_op jit(solution)/shard_map/psum | solution.py:60
  378.7 3.6 multiply_convert_fusion
  382.3 5.0 %convolution_bitcast_fusion = f32[4,16,8,1,2304]{4,2,0,1,3:T(8,128)S(1)} fusion(bf16[16,4,8,1024]{3,2,1,0:T(8,128)(2,1)S(1)} %bitcast.65, bf16[1,2304,1024]{2,1,0:T(8,128)(2,1)} %param.8), kind=kOutput, calls=%fused_computation | convolution fusion | flops 2415919104 | bytes 10485760 | tf_op jit(solution)/shard_map/tf,ldf->tld/dot_general | solution.py:64
  387.3 0.4 copy.11
  387.7 58.9 %all_to_all.21 = f32[4,16,8,1,2304]{4,2,1,3,0:T(8,128)} all-to-all(f32[4,16,8,1,2304]{4,2,1,3,0:T(8,128)S(1)} %copy.11), channel_id=1, replica_groups=mesh['layer'=4,'feat_0'=4,'feat_1'=4,'feat_2'=4] {'feat_2'}, dimensions={0} | all-to-all | bytes 9437184 | tf_op jit(solution)/shard_map/all_to_all | solution.py:18
  446.6 2.7 reduce_sum.58
  449.4 40.7 %all_to_all.22 = f32[16,8,1,2304]{3,1,2,0:T(8,128)S(1)} all-to-all(f32[16,8,1,2304]{3,1,2,0:T(8,128)S(1)} %bitcast.64), channel_id=1, replica_groups=mesh['layer'=4,'feat_0'=4,'feat_1'=4,'feat_2'=4] {'feat_0','feat_1'}, dimensions={0} | all-to-all | bytes 2359296 | tf_op jit(solution)/shard_map/all_to_all | solution.py:26
  490.1 0.8 fusion.20
  490.9 0.5 multiply_bitcast_fusion
  (20 shorter events, 0.6 us)
Async XLA Ops:
  7.2 84.8 %all-gather.3.cloned.1.call-start = ((), (), s32[]{:S(2)}) async-start(), calls=%async_computation.4 | async-start | bytes 2396160 | tf_op jit(solution)/shard_map/all_gather | solution.py:34
  7.9 135.5 %copy-start.2 = (f32[1024]{0:T(1024)S(1)}, f32[1024]{0:T(1024)}, u32[]{:S(2)}) copy-start(f32[1024]{0:T(1024)} %param.11) | copy-start | bytes 12292
  7.9 135.5 %copy-start.3 = (f32[1024]{0:T(1024)S(1)}, f32[1024]{0:T(1024)}, u32[]{:S(2)}) copy-start(f32[1024]{0:T(1024)} %param.10) | copy-start | bytes 12292
  7.9 135.4 %all-reduce.3.cloned.1.call-start = ((), (), s32[]{:S(2)}) async-start(), calls=%async_computation.5 | async-start | bytes 2097152 | tf_op jit(solution)/shard_map/psum | solution.py:38
  213.3 9.3 %copy-start.4 = (f32[1,2304]{1,0:T(1,128)S(1)}, f32[1,2304]{1,0:T(1,128)}, u32[]{:S(2)}) copy-start(f32[1,2304]{1,0:T(1,128)} %param.12) | copy-start | bytes 27652
  213.3 41.2 %copy-start.1 = (bf16[8,1,2304]{2,0,1:T(8,128)(2,1)S(1)}, bf16[8,1,2304]{2,0,1:T(8,128)(2,1)}, u32[]{:S(2)}) copy-start(bf16[8,1,2304]{2,0,1:T(8,128)(2,1)} %param.7) | copy-start | bytes 110596
  213.3 41.1 %all-to-all-start.1 = ((f32[16,8,1,2304]{3,1,2,0:T(8,128)}), f32[16,8,1,2304]{3,1,2,0:T(8,128)S(1)}, u32[]{:S(2)}, u32[]{:S(2)}) async-start(f32[16,8,1,2304]{3,1,2,0:T(8,128)} %bitcast.8), calls=%async_computation.1 | async-start | bytes 2359296 | tf_op jit(solution)/shard_map/all_to_all | solution.py:26
  222.5 104.7 %all-gather.5.cloned.1.call-start = ((), (), s32[]{:S(2)}) async-start(), calls=%async_computation.6 | async-start | bytes 2396160 | tf_op jit(solution)/shard_map/all_gather | solution.py:55
  255.2 123.4 %copy-start = (bf16[512,1024]{1,0:T(8,128)(2,1)S(1)}, bf16[512,1024]{1,0:T(8,128)(2,1)}, u32[]{:S(2)}) copy-start(bf16[512,1024]{1,0:T(8,128)(2,1)} %all-reduce.3.cloned.1.call-done) | copy-start | bytes 3145732
  255.2 123.4 %all-reduce.5.cloned.1.call-start = ((), (), s32[]{:S(2)}) async-start(), calls=%async_computation.7 | async-start | bytes 2097152 | tf_op jit(solution)/shard_map/psum | solution.py:60
Sparse Core Ops, SparseCore 0:
  11.2 80.7 all-gather.2
  98.7 44.6 all-reduce.2
  255.3 71.8 all-gather.4
  334.1 44.5 all-reduce.4
where the time goes:
time: 499 us; the launch traced here: 498 us
  waiting for transfers between devices  277 us (56%)
  blocking collectives  159 us (32%)
  matrix products  23.2 us (5%)
  other arithmetic  14.9 us (3%)
  between operations  13.9 us (3%)
  starting transfers between devices  9.54 us (2%)
    all_to_all x2, blocking collectives, sent_and_summed(): parts = lax.all_to_all(split_up(array, dim, length), axis, 0, 0, tiled=True)  118 us
    all_gather x1, waiting for transfers between devices, shards(): lax.all_gather(activations, FEAT, axis=0, tiled=True)  84 us
    all_gather x1, waiting for transfers between devices, shards(): lax.all_gather(error.astype(jnp.bfloat16), FEAT, axis=0, tiled=True)  71.8 us
    psum x1, waiting for transfers between devices, shards(): lax.psum(partial_value.astype(jnp.bfloat16), 'layer').astype(jnp.float32)  44.8 us
    psum x1, waiting for transfers between devices, shards(): lax.psum(grad_part.astype(jnp.bfloat16), 'layer').astype(jnp.float32)  44.7 us
    all_to_all x1, blocking collectives, sum_by_axis(): lax.all_to_all(nearer, far, split_axis=0, concat_axis=0, tiled=True)  40.7 us
    all_to_all x1, waiting for transfers between devices, sum_by_axis(): lax.all_to_all(nearer, far, split_axis=0, concat_axis=0, tiled=True)  31 us
  transfers between devices with their start and end apart: 5, of which 5 were waited for; matrix products, arithmetic and copies ran while one was open for 0% of the time, Pallas kernels for 0%

commit v1 on v0

--- a/solution.py
+++ b/solution.py
@@ -57,7 +57,9 @@
         preferred_element_type=jnp.float32,
     )
     squared_error = jnp.mean(error * error, axis=-1)
-    latent_grad = lax.psum(grad_part.astype(jnp.bfloat16), "layer").astype(jnp.float32)
+    latent_grad = jnp.sum(lax.all_gather(grad_part.astype(jnp.bfloat16), "layer"), axis=0).astype(
+        jnp.float32
+    )
     preact_grad = (latent_grad * gate_slope).astype(jnp.bfloat16)
     rows = preact_grad
     grad_terms = sum_by_axis(

time: 499 us -> 505 us (1.012)
    all_gather x0 -> x1, waiting for transfers between devices: none -> 46.7 us  [shards(): lax.all_gather(grad_part.astype(jnp.bfloat16), 'layer')]
    psum x1 -> x0, waiting for transfers between devices: 44.7 us -> none  [shards(): lax.psum(grad_part.astype(jnp.bfloat16), 'layer').astype(jnp.float32)]
where the time goes in v1:
time: 505 us; the launch traced here: 504 us
  waiting for transfers between devices  279 us (55%)
  blocking collectives  161 us (32%)
  matrix products  23.2 us (5%)
  other arithmetic  17.1 us (3%)
  between operations  13.9 us (3%)
  starting transfers between devices  9.54 us (2%)
    all_to_all x2, blocking collectives, sent_and_summed(): parts = lax.all_to_all(split_up(array, dim, length), axis, 0, 0, tiled=True)  119 us
    all_gather x1, waiting for transfers between devices, shards(): lax.all_gather(activations, FEAT, axis=0, tiled=True)  84 us
    all_gather x1, waiting for transfers between devices, shards(): lax.all_gather(error.astype(jnp.bfloat16), FEAT, axis=0, tiled=True)  71.8 us
    all_gather x1, waiting for transfers between devices, shards(): lax.all_gather(grad_part.astype(jnp.bfloat16), 'layer')  46.7 us
    psum x1, waiting for transfers between devices, shards(): lax.psum(partial_value.astype(jnp.bfloat16), 'layer').astype(jnp.float32)  44.8 us
    all_to_all x1, blocking collectives, sum_by_axis(): lax.all_to_all(nearer, far, split_axis=0, concat_axis=0, tiled=True)  41.9 us
    all_to_all x1, waiting for transfers between devices, sum_by_axis(): lax.all_to_all(nearer, far, split_axis=0, concat_axis=0, tiled=True)  31 us
  transfers between devices with their start and end apart: 5, of which 5 were waited for; matrix products, arithmetic and copies ran while one was open for 0% of the time, Pallas kernels for 0%

profile of v1, /device:TPU:32, one launch (start us, length us, event | category | flops | bytes accessed | tf_op | source)
XLA Modules:
  0.0 504.1 jit_solution(9363197693395794394)
XLA Ops:
  7.2 0.7 all-gather.5.cloned.1.call-update
  8.0 84.0 %all-gather.5.cloned.1.call-done = bf16[512,1,2304]{2,0,1:T(8,128)(2,1)} async-done(((bf16[8,1,2304]{2,0,1:T(8,128)(2,1)}), bf16[512,1,2304]{2,0,1:T(8,128)(2,1)}) %all-gather.5.cloned.1.call-update) | async-done | bytes 2359312 | tf_op jit(solution)/shard_map/all_gather | solution.py:34
  91.9 6.6 %fusion.10 = bf16[512,1024]{1,0:T(8,128)(2,1)} fusion(bf16[1,2304,1024]{2,1,0:T(8,128)(2,1)} %param.8, bf16[512,1,2304]{2,0,1:T(8,128)(2,1)} %all-gather.5.cloned.1.call-done), kind=kOutput, calls=%fused_computation.15 | convolution fusion | flops 2416443392 | bytes 8126464 | tf_op jit(solution)/shard_map/tld,ldf->tf/dot_general | solution.py:32
  98.6 44.8 %all-reduce.2.cloned.1.call-done = bf16[512,1024]{1,0:T(8,128)(2,1)} async-done(((bf16[512,1024]{1,0:T(8,128)(2,1)}), bf16[512,1024]{1,0:T(8,128)(2,1)}) %all-reduce.2.cloned.1.call-update) | async-done | bytes 1048592 | tf_op jit(solution)/shard_map/psum | solution.py:38
  143.4 1.9 fusion.9
  145.3 4.9 convolution_bitcast_fusion.1
  150.2 0.4 copy.10
  150.6 58.9 %all_to_all.20 = f32[4,16,8,1,2304]{4,2,1,3,0:T(8,128)} all-to-all(f32[4,16,8,1,2304]{4,2,1,3,0:T(8,128)S(1)} %copy.10), channel_id=1, replica_groups=mesh['layer'=4,'feat_0'=4,'feat_1'=4,'feat_2'=4] {'feat_2'}, dimensions={0} | all-to-all | bytes 9437184 | tf_op jit(solution)/shard_map/all_to_all | solution.py:18
  209.6 3.7 reduce_sum.65
  213.3 9.2 %all-to-all-start.1 = ((f32[16,8,1,2304]{3,1,2,0:T(8,128)}), f32[16,8,1,2304]{3,1,2,0:T(8,128)S(1)}, u32[]{:S(2)}, u32[]{:S(2)}) async-start(f32[16,8,1,2304]{3,1,2,0:T(8,128)} %bitcast.8), calls=%async_computation.1 | async-start | bytes 2359296 | tf_op jit(solution)/shard_map/all_to_all | solution.py:26
  222.6 0.8 dynamic-slice_convert_fusion
  223.4 31.0 %all-to-all-done.1 = f32[16,8,1,2304]{3,1,2,0:T(8,128)S(1)} async-done(((f32[16,8,1,2304]{3,1,2,0:T(8,128)}), f32[16,8,1,2304]{3,1,2,0:T(8,128)S(1)}, u32[]{:S(2)}, u32[]{:S(2)}) %all-to-all-start.1) | async-done | bytes 1179680 | tf_op jit(solution)/shard_map/all_to_all | solution.py:26
  254.5 0.7 fusion.23
  255.4 71.8 %all-gather.7.cloned.1.call-done = bf16[512,1,2304]{2,0,1:T(8,128)(2,1)} async-done(((bf16[8,1,2304]{2,0,1:T(8,128)(2,1)}), bf16[512,1,2304]{2,0,1:T(8,128)(2,1)}) %all-gather.7.cloned.1.call-update) | async-done | bytes 2359312 | tf_op jit(solution)/shard_map/all_gather | solution.py:55
  327.3 6.7 %fusion.15 = bf16[512,1024]{1,0:T(8,128)(2,1)} fusion(bf16[1,1024,2304]{2,1,0:T(8,128)(2,1)} %param.9, bf16[512,1,2304]{2,0,1:T(8,128)(2,1)} %all-gather.7.cloned.1.call-done), kind=kOutput, calls=%fused_computation.16 | convolution fusion | flops 2416443392 | bytes 8126464 | tf_op jit(solution)/shard_map/tld,lfd->tf/dot_general | solution.py:53
  333.9 46.7 %all-gather.9.cloned.1.call-done = bf16[2048,1024]{1,0:T(8,128)(2,1)} async-done(((bf16[512,1024]{1,0:T(8,128)(2,1)}), bf16[2048,1024]{1,0:T(8,128)(2,1)}) %all-gather.9.cloned.1.call-update) | async-done | bytes 4194320 | tf_op jit(solution)/shard_map/all_gather | solution.py:60
  380.6 3.4 reduce_sum.70
  384.0 2.4 multiply_convert_fusion
  386.4 5.0 convolution_bitcast_fusion
  391.8 59.7 %all_to_all.21 = f32[4,16,8,1,2304]{4,2,1,3,0:T(8,128)} all-to-all(f32[4,16,8,1,2304]{4,2,1,3,0:T(8,128)S(1)} %copy.11), channel_id=1, replica_groups=mesh['layer'=4,'feat_0'=4,'feat_1'=4,'feat_2'=4] {'feat_2'}, dimensions={0} | all-to-all | bytes 9437184 | tf_op jit(solution)/shard_map/all_to_all | solution.py:18
  451.5 2.7 reduce_sum.71
  454.3 41.9 %all_to_all.22 = f32[16,8,1,2304]{3,1,2,0:T(8,128)S(1)} all-to-all(f32[16,8,1,2304]{3,1,2,0:T(8,128)S(1)} %bitcast.65), channel_id=1, replica_groups=mesh['layer'=4,'feat_0'=4,'feat_1'=4,'feat_2'=4] {'feat_0','feat_1'}, dimensions={0} | all-to-all | bytes 2359296 | tf_op jit(solution)/shard_map/all_to_all | solution.py:26
  496.2 0.8 fusion.20
  497.1 0.5 multiply_bitcast_fusion
  (21 shorter events, 1.0 us)
Async XLA Ops:
  7.2 84.8 %all-gather.5.cloned.1.call-start = ((), (), s32[]{:S(2)}) async-start(), calls=%async_computation.4 | async-start | bytes 2396160 | tf_op jit(solution)/shard_map/all_gather | solution.py:34
  7.9 135.5 %copy-start.2 = (f32[1024]{0:T(1024)S(1)}, f32[1024]{0:T(1024)}, u32[]{:S(2)}) copy-start(f32[1024]{0:T(1024)} %param.11) | copy-start | bytes 12292
  7.9 135.5 %copy-start.3 = (f32[1024]{0:T(1024)S(1)}, f32[1024]{0:T(1024)}, u32[]{:S(2)}) copy-start(f32[1024]{0:T(1024)} %param.10) | copy-start | bytes 12292
  7.9 135.4 %all-reduce.2.cloned.1.call-start = ((), (), s32[]{:S(2)}) async-start(), calls=%async_computation.5 | async-start | bytes 2097152 | tf_op jit(solution)/shard_map/psum | solution.py:38
  213.3 9.3 %copy-start.4 = (f32[1,2304]{1,0:T(1,128)S(1)}, f32[1,2304]{1,0:T(1,128)}, u32[]{:S(2)}) copy-start(f32[1,2304]{1,0:T(1,128)} %param.12) | copy-start | bytes 27652
  213.3 41.2 %copy-start.1 = (bf16[8,1,2304]{2,0,1:T(8,128)(2,1)S(1)}, bf16[8,1,2304]{2,0,1:T(8,128)(2,1)}, u32[]{:S(2)}) copy-start(bf16[8,1,2304]{2,0,1:T(8,128)(2,1)} %param.7) | copy-start | bytes 110596
  213.3 41.1 %all-to-all-start.1 = ((f32[16,8,1,2304]{3,1,2,0:T(8,128)}), f32[16,8,1,2304]{3,1,2,0:T(8,128)S(1)}, u32[]{:S(2)}, u32[]{:S(2)}) async-start(f32[16,8,1,2304]{3,1,2,0:T(8,128)} %bitcast.8), calls=%async_computation.1 | async-start | bytes 2359296 | tf_op jit(solution)/shard_map/all_to_all | solution.py:26
  222.5 104.7 %all-gather.7.cloned.1.call-start = ((), (), s32[]{:S(2)}) async-start(), calls=%async_computation.6 | async-start | bytes 2396160 | tf_op jit(solution)/shard_map/all_gather | solution.py:55
  255.2 125.4 %all-gather.9.cloned.1.call-start = ((), (), s32[]{:S(2)}) async-start(), calls=%async_computation.7 | async-start | bytes 5242880 | tf_op jit(solution)/shard_map/all_gather | solution.py:60
  380.6 3.4 copy-start
Sparse Core Ops, SparseCore 0:
  11.2 80.7 all-gather.4
  98.7 44.6 all-reduce.1
  255.3 71.8 all-gather.6
  334.1 46.4 all-gather.8
